TPU v7x, 32 devices: a whole 2x2x4 slice. The times are simulated.
32 devices in a mesh: gx: 8 (over y, x, core), gy: 4 (over z).
Axes of the slice: x: 2, y: 2, z: 4, core: 2. Of those that a mesh axis runs over, the one named last changes fastest.
Arguments:
- node_disp: float32 [2, 256, 1024], P(None, 'gx', 'gy'), may hold values from -0.24 to 0.24
- node_vel: float32 [2, 256, 1024], P(None, 'gx', 'gy'), may hold values from -6 to 6
- node_mass: float32 [256, 1024], P('gx', 'gy'), may hold values from 0.5 to 2
- zone_mass: float32 [256, 1024], P('gx', 'gy'), may hold values from 0.5 to 2
- zone_energy: float32 [256, 1024], P('gx', 'gy'), may hold values from 0.3 to 7.5
- master_block: bfloat16 [32, 4, 1024], P(('gx', 'gy')), may hold values from -3 to 3, as said below
- owner: int32 [1], replicated, may hold values from 0 to 31
- pair_node: int32 [32, 1024], P(('gx', 'gy')), may hold values from 0 to 8191
- pair_segment: int32 [32, 1024], P(('gx', 'gy')), may hold values from 0 to 1022
- pair_side: int32 [32, 1024], P(('gx', 'gy')), may hold values 0 or 1
- pair_count: int32 [32], P(('gx', 'gy')), may hold values from 0 to 1024, as said below
Outputs:
- new_vel: float32 [2, 256, 1024], P(None, 'gx', 'gy')
- new_disp: float32 [2, 256, 1024], P(None, 'gx', 'gy')
- master_impulse: float32 [3, 1024], P(None, ('gx', 'gy'))
Inputs may be any that keep to these rules, and one draw needn't show every extreme that they name: `pair_node`: local node numbers, row-major over a device's 32 x 256 block. `pair_count`: at most 1024; one device has exactly 1024 in every draw; slots at or past a device's count are not pairs. `master_block`: rows 0 and 1 lie within -0.25 to 0.25.
All inputs are finite; a program needn't handle non-finite values. No bound on the sum of `pair_side` on one device may be relied on, other than what follows from the above.
Results may differ from a plain program's by a relative error of at most 0.0015.
Values may be sent and summed in bfloat16 or wider, within the bound.
A program may use at most 128 MiB of HBM per device.

v0:
```python
import jax
import jax.numpy as jnp
from jax import lax
from jax.sharding import PartitionSpec as P

STIFFNESS = 10.0
GAP_SCALE = 0.05


def spread(block, axis, source):
    block = jnp.where(lax.axis_index(axis) == source, block, jnp.zeros_like(block))
    return lax.psum(block, axis)


def with_halo(cells, sides, width):
    for axis, dim in sides:
        count = lax.axis_size(axis)
        ends = count - 1
        head = lax.slice_in_dim(cells, 0, width, axis=dim)
        tail = lax.slice_in_dim(cells, cells.shape[dim] - width, cells.shape[dim], axis=dim)
        cells = jnp.concatenate(
            [
                lax.ppermute(tail, axis, [(i, (i + 1) % count) for i in range(ends)]),
                cells,
                lax.ppermute(head, axis, [((i + 1) % count, i) for i in range(ends)]),
            ],
            axis=dim,
        )
    return cells


def corner_forces(corner_a, corner_b, corner_c, corner_e, zone_load, zone_live):
    first_dx = 1.0 + corner_c[0] - corner_a[0]
    first_dy = 1.0 + corner_c[1] - corner_a[1]
    second_dx = -1.0 + corner_e[0] - corner_b[0]
    second_dy = 1.0 + corner_e[1] - corner_b[1]
    zone_area = 0.5 * (first_dx * second_dy - second_dx * first_dy)
    safe_area = jnp.where(zone_live, zone_area, 1.0)
    half_press = jnp.where(zone_live, 0.2 * zone_load / safe_area, 0.0)
    force_a = jnp.stack([-half_press * second_dy, half_press * second_dx])
    force_b = jnp.stack([half_press * first_dy, -half_press * first_dx])
    return (safe_area, force_a, force_b, -force_a, -force_b)


def contact_terms(slave_disp, seg_start, seg_end, side_flags, live_mask):
    rel_x = slave_disp[0] - seg_start[0] + 0.5
    rel_y = slave_disp[1] - seg_start[1]
    along_x = 1.0 + seg_end[0] - seg_start[0]
    along_y = seg_end[1] - seg_start[1]
    along_sq = along_x * along_x + along_y * along_y
    length = jnp.sqrt(along_sq)
    fraction = (rel_x * along_x + rel_y * along_y) / along_sq
    normal_x = -along_y / length
    normal_y = along_x / length
    gap_size = normal_x * rel_x + normal_y * rel_y
    side_sign = 1.0 - 2.0 * side_flags.astype(jnp.float32)
    magnitude = jnp.where(
        live_mask, STIFFNESS * GAP_SCALE * jax.nn.softplus(-side_sign * gap_size / GAP_SCALE), 0.0
    )
    slave_push = jnp.stack([magnitude * side_sign * normal_x, magnitude * side_sign * normal_y])
    react_first = jnp.stack(
        [
            -(1.0 - fraction) * slave_push[0],
            -(1.0 - fraction) * slave_push[1],
            (1.0 - fraction) * magnitude,
        ]
    )
    react_second = jnp.stack(
        [-fraction * slave_push[0], -fraction * slave_push[1], fraction * magnitude]
    )
    return (slave_push, react_first, react_second)


def shards(
    node_disp,
    node_vel,
    node_mass,
    zone_mass,
    zone_energy,
    master_block,
    owner,
    pair_node,
    pair_segment,
    pair_side,
    pair_count,
):
    row_count = node_disp.shape[1]
    col_count = node_disp.shape[2]
    row_base = lax.axis_index("gx") * row_count
    col_base = lax.axis_index("gy") * col_count
    total_rows = row_count * lax.axis_size("gx")
    total_cols = col_count * lax.axis_size("gy")
    surface = spread(master_block[0], ("gx", "gy"), owner[0])
    packed = jnp.concatenate([node_disp, (zone_energy * zone_mass)[None]], axis=0)
    extended = with_halo(packed.astype(jnp.bfloat16), (("gx", 1), ("gy", 2)), 1).astype(
        packed.dtype
    )
    zone_rows = row_base - 1 + jnp.arange(row_count + 1, dtype=jnp.int32)
    zone_cols = col_base - 1 + jnp.arange(col_count + 1, dtype=jnp.int32)
    zone_live = (
        (zone_rows[:, None] >= 0)
        & (zone_rows[:, None] < total_rows - 1)
        & (zone_cols[None, :] >= 0)
        & (zone_cols[None, :] < total_cols - 1)
    )
    safe_area, force_a, force_b, force_c, force_e = corner_forces(
        extended[:2, : row_count + 1, : col_count + 1],
        extended[:2, 1:, : col_count + 1],
        extended[:2, 1:, 1:],
        extended[:2, : row_count + 1, 1:],
        extended[2, : row_count + 1, : col_count + 1],
        zone_live,
    )
    node_force = (
        force_a[:, 1:, 1:]
        + force_b[:, :row_count, 1:]
        + force_c[:, :row_count, :col_count]
        + force_e[:, 1:, :col_count]
    )
    own_area = safe_area[1:, 1:]
    own_live = zone_live[1:, 1:]
    zone_ratio = jnp.where(own_live, jnp.sqrt(own_area) / jnp.sqrt(0.56 * zone_energy), 1e30)
    step_size = 0.3 * lax.pmin(jnp.min(zone_ratio), ("gx", "gy"))
    coords = surface[0:2].astype(jnp.float32)
    flat_disp = node_disp.reshape(2, row_count * col_count)
    live_count = pair_count[0]
    block_count = (live_count + 127) // 128
    surface_nodes = surface.shape[1]

    def contact_block(block_index, loop_state):
        pushed, reaction = loop_state
        first_pair = block_index * 128
        slave_nodes = lax.dynamic_slice_in_dim(pair_node[0], first_pair, 128)
        segment_ids = lax.dynamic_slice_in_dim(pair_segment[0], first_pair, 128)
        side_flags = lax.dynamic_slice_in_dim(pair_side[0], first_pair, 128)
        live_mask = first_pair + jnp.arange(128, dtype=jnp.int32) < live_count
        slave_disp = jnp.take(flat_disp, slave_nodes, axis=1)
        seg_start = jnp.take(coords, segment_ids, axis=1)
        seg_end = jnp.take(coords, segment_ids + 1, axis=1)
        slave_push, react_first, react_second = contact_terms(
            slave_disp, seg_start, seg_end, side_flags, live_mask
        )
        pushed = pushed.at[:, slave_nodes].add(slave_push)
        reaction = (
            reaction.at[:, segment_ids].add(react_first).at[:, segment_ids + 1].add(react_second)
        )
        return (pushed, reaction)

    pushed, reaction = lax.fori_loop(
        0,
        block_count,
        contact_block,
        (
            jnp.zeros((2, row_count * col_count), jnp.float32),
            jnp.zeros((3, surface_nodes), jnp.float32),
        ),
    )
    total_force = node_force + pushed.reshape(2, row_count, col_count)
    new_vel = node_vel + step_size * total_force / node_mass
    new_disp = node_disp + step_size * new_vel
    share_width = surface_nodes // (lax.axis_size("gx") * lax.axis_size("gy"))
    my_index = lax.axis_index("gx") * lax.axis_size("gy") + lax.axis_index("gy")
    summed = lax.psum(reaction, ("gx", "gy"))
    reaction_share = lax.dynamic_slice_in_dim(summed, my_index * share_width, share_width, 1)
    prior_impulse = lax.dynamic_slice_in_dim(
        surface[2:4], my_index * share_width, share_width, 1
    ).astype(jnp.float32)
    master_impulse = jnp.concatenate(
        [prior_impulse + step_size * reaction_share[0:2], step_size * reaction_share[2:3]], axis=0
    )
    return (new_vel, new_disp, master_impulse)


def solution(mesh):
    in_specs = (
        P(None, "gx", "gy"),
        P(None, "gx", "gy"),
        P("gx", "gy"),
        P("gx", "gy"),
        P("gx", "gy"),
        P(("gx", "gy"), None, None),
        P(),
        P(("gx", "gy"), None),
        P(("gx", "gy"), None),
        P(("gx", "gy"), None),
        P(("gx", "gy")),
    )
    out_specs = (P(None, "gx", "gy"), P(None, "gx", "gy"), P(None, ("gx", "gy")))
    return jax.shard_map(shards, mesh=mesh, in_specs=in_specs, out_specs=out_specs, check_vma=False)
```

profile of v0, /device:TPU:0, one launch (start us, length us, event | category | flops | bytes accessed | tf_op | source)
XLA Modules:
  0.0 284.9 jit_solution(1729171996044898759)
XLA Ops:
  0.6 0.9 convert.7
  1.5 0.8 fusion.25
  2.3 2.4 collective-permute-start
  4.7 1.3 collective-permute-start.1
  6.6 3.4 %copy.43 = f32[2,32,256]{0,2,1:T(8,128)} copy(f32[2,32,256]{2,1,0:T(8,128)} %param.15) | data formatting | bytes 131072 | tf_op args[0]
  10.7 44.0 %psum.14 = bf16[4,1024]{1,0:T(4,128)(2,1)S(1)} all-reduce(bf16[4,1024]{1,0:T(4,128)(2,1)S(1)} %select_bitcast_fusion.3), channel_id=1, replica_groups=mesh['gx'=8,'gy'=4] {'gx','gy'}, use_global_device_ids=true, to_apply=%region_2.3 | all-reduce | flops 4096 | bytes 16384 | tf_op jit(solution)/shard_map/psum | solution.py:12
  54.9 2.2 broadcast_in_dim.60
  57.2 34.1 %while.14 = (s32[]{:T(128)}, f32[2,8192]{0,1:T(8,128)}, f32[3,1024]{0,1:T(8,128)S(1)}, s32[]{:T(128)}, s32[1,1024]{1,0:T(1,128)}, /*index=5*/s32[]{:T(128)}, s32...) while((s32[]{:T(128)}, f32[2,8192]{0,1:T(8,128)}, ...), condition=%wide.region_7.9_spmd, body=%wide.region_3.8_spmd.sunk | while | flops 17542 | bytes 83919 | solution.py:149
  57.2 0.7 fusion.36
  58.6 2.8 gather_fusion.2
  61.5 0.7 compare_and_fusion.5
  63.6 1.4 negate_multiply_fusion.9
  65.0 0.7 negate_multiply_fusion.10
  65.8 5.3 %scatter_fusion = f32[2,8192]{0,1:T(8,128)} fusion(f32[2,8192]{0,1:T(8,128)} %get-tuple-element.335, s32[128]{0:T(128)S(1)} %get-tuple-element.302, f32[128,2]{1,0:T(8,128)S(1)} %copy.57), kind=kCustom, calls=%fused_computation.3.clone.1 | custom fusion | flops 256 | bytes 3584 | tf_op jit(solution)/shard_map/while/body/scatter-add | solution.py:143
  71.2 1.5 scatter_fusion.1
  72.8 1.5 scatter_fusion.2
  74.3 0.7 fusion.36
  75.6 2.8 gather_fusion.2
  78.5 0.7 compare_and_fusion.5
  80.7 1.4 negate_multiply_fusion.9
  82.1 0.7 negate_multiply_fusion.10
  82.9 5.3 %scatter_fusion = f32[2,8192]{0,1:T(8,128)} fusion(f32[2,8192]{0,1:T(8,128)} %get-tuple-element.335, s32[128]{0:T(128)S(1)} %get-tuple-element.302, f32[128,2]{1,0:T(8,128)S(1)} %copy.57), kind=kCustom, calls=%fused_computation.3.clone.1 | custom fusion | flops 256 | bytes 3584 | tf_op jit(solution)/shard_map/while/body/scatter-add | solution.py:143
  88.3 1.5 scatter_fusion.1
  89.9 1.5 scatter_fusion.2
  91.7 137.8 %psum.15 = f32[3,1024]{1,0:T(4,128)S(1)} all-reduce(f32[3,1024]{1,0:T(4,128)S(1)} %copy.46), channel_id=1, replica_groups=mesh['gx'=8,'gy'=4] {'gx','gy'}, use_global_device_ids=true, to_apply=%region_8.10 | all-reduce | flops 3072 | bytes 24576 | tf_op jit(solution)/shard_map/psum | solution.py:163
  229.6 2.8 collective-permute-start.2
  232.4 1.3 collective-permute-start.3
  234.0 4.2 %collective-permute-done.3 = bf16[3,34,1]{2,1,0:T(8,128)(2,1)S(1)} collective-permute-done((bf16[3,34,1]{2,1,0:T(8,128)(2,1)S(1)}, bf16[3,34,1]{2,1,0:T(8,128)(2,1)S(1)}, u32[]{:S(2)}, u32[]{:S(2)}) %collective-permute-start.3) | collective-permute-done | bytes 236 | tf_op jit(solution)/shard_map/ppermute | solution.py:25
  238.5 0.7 fusion.24
  239.2 2.8 copy.47
  242.0 40.6 %pmin.7 = f32[]{:T(128)} all-reduce(f32[]{:T(128)} %fusion.24), channel_id=1, replica_groups=mesh['gx'=8,'gy'=4] {'gx','gy'}, use_global_device_ids=true, to_apply=%region_1.2 | all-reduce | flops 1 | bytes 8 | tf_op jit(solution)/shard_map/pmin | solution.py:123
  284.1 0.8 multiply_add_fusion.1
  (71 shorter events, 7.1 us)
Async XLA Ops:
  0.6 10.0 %copy-start.4 = (bf16[1,4,1024]{2,1,0:T(4,128)(2,1)S(1)}, bf16[1,4,1024]{2,1,0:T(4,128)(2,1)}, u32[]{:S(2)}) copy-start(bf16[1,4,1024]{2,1,0:T(4,128)(2,1)} %param.20) | copy-start | bytes 24580
  2.3 227.2 %collective-permute-start = (bf16[3,1,256]{2,1,0:T(2,128)(2,1)S(1)}, bf16[3,1,256]{2,1,0:T(2,128)(2,1)S(1)}, u32[]{:S(2)}, u32[]{:S(2)}) collective-permute-start(bf16[3,1,256]{2,1,0:T(2,128)(2,1)S(1)} %get-tuple-element.214), channel_id=1, source_target_pairs={{0,4},{4,8},{8,12},{12,16},{16,20},{20,24},{24,28},{1,5},{5,9},{9,... | collective-permute-start | bytes 4616 | tf_op jit(solution)/shard_map/ppermute | solution.py:23
  4.7 224.8 %collective-permute-start.1 = (bf16[3,1,256]{2,1,0:T(2,128)(2,1)S(1)}, bf16[3,1,256]{2,1,0:T(2,128)(2,1)S(1)}, u32[]{:S(2)}, u32[]{:S(2)}) collective-permute-start(bf16[3,1,256]{2,1,0:T(2,128)(2,1)S(1)} %get-tuple-element.215), channel_id=1, source_target_pairs={{4,0},{8,4},{12,8},{16,12},{20,16},{24,20},{28,24},{5,1},{9,5},{13... | collective-permute-start | bytes 4616 | tf_op jit(solution)/shard_map/ppermute | solution.py:25
  54.9 183.6 %copy-start.1 = (f32[32,256]{1,0:T(8,128)S(1)}, f32[32,256]{1,0:T(8,128)}, u32[]{:S(2)}) copy-start(f32[32,256]{1,0:T(8,128)} %param.19) | copy-start | bytes 98308
  91.4 192.8 %copy-start = (f32[2,32,256]{2,1,0:T(8,128)S(1)}, f32[2,32,256]{2,1,0:T(8,128)}, u32[]{:S(2)}) copy-start(f32[2,32,256]{2,1,0:T(8,128)} %param.15) | copy-start | bytes 196612
  91.4 192.7 %copy-start.2 = (f32[2,32,256]{2,1,0:T(8,128)S(1)}, f32[2,32,256]{2,1,0:T(8,128)}, u32[]{:S(2)}) copy-start(f32[2,32,256]{2,1,0:T(8,128)} %param.16) | copy-start | bytes 196612
  91.4 192.7 %copy-start.3 = (f32[32,256]{1,0:T(8,128)S(1)}, f32[32,256]{1,0:T(8,128)}, u32[]{:S(2)}) copy-start(f32[32,256]{1,0:T(8,128)} %param.17) | copy-start | bytes 98308
  229.6 4.4 %collective-permute-start.2 = (bf16[3,34,1]{2,1,0:T(8,128)(2,1)S(1)}, bf16[3,34,1]{2,1,0:T(8,128)(2,1)S(1)}, u32[]{:S(2)}, u32[]{:S(2)}) collective-permute-start(bf16[3,34,1]{2,1,0:T(8,128)(2,1)S(1)} %get-tuple-element.212), channel_id=1, source_target_pairs={{0,1},{1,2},{2,3},{4,5},{5,6},{6,7},{8,9},{9,10},{10,11},{12,13},{... | collective-permute-start | bytes 620 | tf_op jit(solution)/shard_map/ppermute | solution.py:23
  232.4 5.8 %collective-permute-start.3 = (bf16[3,34,1]{2,1,0:T(8,128)(2,1)S(1)}, bf16[3,34,1]{2,1,0:T(8,128)(2,1)S(1)}, u32[]{:S(2)}, u32[]{:S(2)}) collective-permute-start(bf16[3,34,1]{2,1,0:T(8,128)(2,1)S(1)} %get-tuple-element.213), channel_id=1, source_target_pairs={{1,0},{2,1},{3,2},{5,4},{6,5},{7,6},{9,8},{10,9},{11,10},{13,12},{... | collective-permute-start | bytes 620 | tf_op jit(solution)/shard_map/ppermute | solution.py:25
where the time goes:
time: 288 us; the launch traced here: 285 us
  blocking collectives  222 us (77%)
  other arithmetic  29 us (10%)
  local copies, waits for them, and re-layouts  18.4 us (6%)
  starting transfers between devices  7.77 us (3%)
  waiting for transfers between devices  4.41 us (2%)
    psum x1, blocking collectives, shards(): summed = lax.psum(reaction, ('gx', 'gy'))  138 us
    psum x1, blocking collectives, spread(): return lax.psum(block, axis)  44 us
    pmin x1, blocking collectives, shards(): step_size = 0.3 * lax.pmin(jnp.min(zone_ratio), ('gx', 'gy'))  40.6 us
    scatter-add x2, other arithmetic, contact_block(): pushed = pushed.at[:, slave_nodes].add(slave_push)  10.6 us
    scatter-add x4, other arithmetic, contact_block(): reaction.at[:, segment_ids].add(react_first).at[:, segment_ids + 1]  5.81 us
    gather x4, local copies, waits for them, and re-layouts, contact_block(): slave_disp = jnp.take(flat_disp, slave_nodes, axis=1)  5.79 us
  transfers between devices with their start and end apart: 4, of which 2 were waited for; matrix products, arithmetic and copies ran while one was open for 14% of the time, Pallas kernels for 0%

commit v1 on v0

v1 whole, which is shorter than its diff:
```python
import functools

import jax
import jax.numpy as jnp
from jax import lax
from jax.experimental import pallas as pl
from jax.experimental.pallas import tpu as pltpu
from jax.sharding import PartitionSpec as P

STIFFNESS = 10.0
GAP_SCALE = 0.05
MESH = pl.DeviceIdType.MESH
F32 = jnp.float32
BF16 = jnp.bfloat16


def two_parts(value):
    top = value.astype(BF16).astype(F32)
    return top, value - top


def dot_nt(left, right):
    return lax.dot_general(left, right, (((1,), (1,)), ((), ())), preferred_element_type=F32)


def rolled(value, shift, axis):
    return pltpu.roll(value, shift % value.shape[axis], axis)


def step_kernel(
    n_gx, n_gy,
    owner_ref, count_ref, disp_in, vel_in, mass_in, zmass_in, energy_in, block_in, node_in, seg_in, side_in,
    vel_out, disp_out, imp_out,
    disp, vel, mass, zmass, energy, block, node, seg, side,
    new_vel, new_disp, new_imp,
    up_pack, down_pack, left_pack, right_pack,
    from_down, from_up, from_right, from_left,
    plane_slots, line_send, line_slots, table,
    oh_col, oh_lo, oh_share, early, early_in, react, react_in,
    in_sem, out_sem, halo_send, halo_recv,
    plane_send_sem, plane_recv_sem, line_send_sem, line_recv_sem,
    early_send_sem, early_recv_sem, react_send_sem, react_recv_sem,
):
    n = n_gx * n_gy
    mx, my = lax.axis_index("gx"), lax.axis_index("gy")
    me = mx * n_gy + my
    rows, cols = disp.shape[1], disp.shape[2]
    pairs = node.shape[1]
    mnodes = block.shape[2]
    share = mnodes // n
    groups = mnodes // 128

    loads = [
        pltpu.make_async_copy(src, dst, in_sem.at[i])
        for i, (src, dst) in enumerate(
            [(block_in, block), (node_in, node), (disp_in, disp), (seg_in, seg), (energy_in, energy),
             (zmass_in, zmass), (side_in, side), (mass_in, mass), (vel_in, vel)]
        )
    ]
    for load in loads:
        load.start()
    for ref in (from_down, from_up, from_right, from_left):
        ref[...] = jnp.zeros(ref.shape, F32)

    barrier = pltpu.get_barrier_semaphore()
    for d in range(1, n_gx):
        pl.semaphore_signal(barrier, inc=1, device_id=(lax.rem(mx + d, n_gx), my), device_id_type=MESH)
    for d in range(1, n_gy):
        pl.semaphore_signal(barrier, inc=1, device_id=(mx, lax.rem(my + d, n_gy)), device_id_type=MESH)

    for load in loads[:7]:
        load.wait()

    dx, dy = disp[0], disp[1]
    zload = energy[...] * zmass[...]
    sub = lax.broadcasted_iota(jnp.int32, (8, cols), 0)
    up_pack[...] = jnp.where(sub == 0, dx[:8], jnp.where(sub == 1, rolled(dy[:8], 1, 0), 0.0))
    tail = slice(rows - 8, rows)
    down_pack[...] = jnp.where(
        sub == 7, dx[tail],
        jnp.where(sub == 6, rolled(dy[tail], -1, 0), jnp.where(sub == 5, rolled(zload[tail], -2, 0), 0.0)),
    )
    plane_slots[mx] = block[0, 0:2]

    node_id = node[...]
    seg_id = seg[...]
    seg_next = seg_id + 1
    node_row, node_col = node_id // cols, node_id % cols
    oh_col[...] = (lax.broadcasted_iota(jnp.int32, (cols, pairs), 0) == node_col).astype(F32).astype(BF16)
    oh_lo[...] = (lax.broadcasted_iota(jnp.int32, (128, pairs), 0) == seg_id % 128).astype(F32).astype(BF16)
    share_iota = lax.broadcasted_iota(jnp.int32, (n, pairs), 0)
    oh_share[:, :pairs] = (share_iota == seg_id // share).astype(F32).astype(BF16)
    oh_share[:, pairs:] = (share_iota == seg_next // share).astype(F32).astype(BF16)
    row_mask = lax.broadcasted_iota(jnp.int32, (rows, pairs), 0) == node_row

    flat = disp[...].reshape(2 * rows, cols)
    flat_top, flat_low = two_parts(flat)
    looked = jnp.dot(
        jnp.concatenate([flat_top, flat_low], axis=0).astype(BF16), oh_col[...], preferred_element_type=F32
    )
    looked = looked[: 2 * rows] + looked[2 * rows:]
    slave_x = jnp.sum(jnp.where(row_mask, looked[:rows], 0.0), axis=0, keepdims=True)
    slave_y = jnp.sum(jnp.where(row_mask, looked[rows:], 0.0), axis=0, keepdims=True)

    owner = owner_ref[0]
    master_id = lax.broadcasted_iota(jnp.int32, (1, mnodes), 1)
    prior = jnp.where(owner == me, block[0, 2:4].astype(F32), 0.0)
    prior_mask = lax.broadcasted_iota(jnp.int32, (share, mnodes), 0) == master_id % share
    prior_cols = jnp.concatenate(
        [jnp.where(prior_mask, prior[0:1], 0.0), jnp.where(prior_mask, prior[1:2], 0.0),
         jnp.zeros((128 - 2 * share, mnodes), F32)], axis=0
    ).astype(BF16)
    prior_rows = (lax.broadcasted_iota(jnp.int32, (n, mnodes), 0) == master_id // share).astype(F32).astype(BF16)
    early[...] = dot_nt(prior_rows, prior_cols)

    pl.semaphore_wait(barrier, n_gx + n_gy - 2)

    plane_copies = []
    for d in range(1, n_gx):
        plane_copies.append(pltpu.make_async_remote_copy(
            src_ref=plane_slots.at[mx], dst_ref=plane_slots.at[mx],
            send_sem=plane_send_sem.at[d], recv_sem=plane_recv_sem.at[d],
            device_id=(lax.rem(mx + d, n_gx), my), device_id_type=MESH))
        plane_copies[-1].start()

    def halo(src, dst, slot, device):
        return pltpu.make_async_remote_copy(
            src_ref=src, dst_ref=dst, send_sem=halo_send.at[slot], recv_sem=halo_recv.at[slot],
            device_id=device, device_id_type=MESH)

    to_up = halo(up_pack, from_down, 0, (jnp.maximum(mx - 1, 0), my))
    to_down = halo(down_pack, from_up, 1, (jnp.minimum(mx + 1, n_gx - 1), my))
    to_left = halo(left_pack, from_right, 2, (mx, jnp.maximum(my - 1, 0)))
    to_right = halo(right_pack, from_left, 3, (mx, jnp.minimum(my + 1, n_gy - 1)))
    has_up, has_down = mx > 0, mx < n_gx - 1
    has_left, has_right = my > 0, my < n_gy - 1

    @pl.when(has_up)
    def _():
        to_up.start()

    @pl.when(has_down)
    def _():
        to_down.start()

    @pl.when(has_down)
    def _():
        to_up.wait_recv()

    @pl.when(has_up)
    def _():
        to_down.wait_recv()

    below, above = from_down[...], from_up[...]
    ext_x = jnp.concatenate([dx, jnp.where(sub < 4, below, above)], axis=0)
    ext_y = jnp.concatenate([dy, jnp.where(sub < 4, rolled(below, -1, 0), rolled(above, 1, 0))], axis=0)
    ext_l = jnp.concatenate([zload, rolled(above, 2, 0)], axis=0)
    lane = lax.broadcasted_iota(jnp.int32, (rows + 8, 128), 1)
    last = slice(cols - 128, cols)
    left_pack[...] = jnp.where(lane == 0, ext_x[:, :128], jnp.where(lane == 1, rolled(ext_y[:, :128], 1, 1), 0.0))
    right_pack[...] = jnp.where(
        lane == 127, ext_x[:, last],
        jnp.where(lane == 126, rolled(ext_y[:, last], -1, 1),
                  jnp.where(lane == 125, rolled(ext_l[:, last], -2, 1), 0.0)),
    )

    @pl.when(has_left)
    def _():
        to_left.start()

    @pl.when(has_right)
    def _():
        to_right.start()

    for d in range(1, n_gx):
        pltpu.make_async_remote_copy(
            src_ref=plane_slots.at[mx], dst_ref=plane_slots.at[lax.rem(mx + n_gx - d, n_gx)],
            send_sem=plane_send_sem.at[d], recv_sem=plane_recv_sem.at[d],
            device_id=(lax.rem(mx + d, n_gx), my), device_id_type=MESH).wait_recv()

    line_slots[my] = plane_slots[owner // n_gy]
    line_copies = []
    for d in range(1, n_gy):
        line_copies.append(pltpu.make_async_remote_copy(
            src_ref=line_slots.at[my], dst_ref=line_slots.at[my],
            send_sem=line_send_sem.at[d], recv_sem=line_recv_sem.at[d],
            device_id=(mx, lax.rem(my + d, n_gy)), device_id_type=MESH))
        line_copies[-1].start()

    @pl.when(has_right)
    def _():
        to_left.wait_recv()

    @pl.when(has_left)
    def _():
        to_right.wait_recv()

    right, left = from_right[...], from_left[...]
    ext_x = jnp.concatenate([ext_x, jnp.where(lane < 64, right, left)], axis=1)
    ext_y = jnp.concatenate([ext_y, jnp.where(lane < 64, rolled(right, -1, 1), rolled(left, 1, 1))], axis=1)
    ext_l = jnp.concatenate([ext_l, rolled(left, 2, 1)], axis=1)
    ext_shape = ext_x.shape
    zone_row = lax.broadcasted_iota(jnp.int32, ext_shape, 0)
    zone_row = jnp.where(zone_row == ext_shape[0] - 1, -1, zone_row) + mx * rows
    zone_col = lax.broadcasted_iota(jnp.int32, ext_shape, 1)
    zone_col = jnp.where(zone_col == ext_shape[1] - 1, -1, zone_col) + my * cols
    live = (zone_row >= 0) & (zone_row < n_gx * rows - 1) & (zone_col >= 0) & (zone_col < n_gy * cols - 1)
    b_x, b_y = rolled(ext_x, -1, 0), rolled(ext_y, -1, 0)
    c_x, c_y = rolled(b_x, -1, 1), rolled(b_y, -1, 1)
    e_x, e_y = rolled(ext_x, -1, 1), rolled(ext_y, -1, 1)
    first_dx, first_dy = 1.0 + c_x - ext_x, 1.0 + c_y - ext_y
    second_dx, second_dy = -1.0 + e_x - b_x, 1.0 + e_y - b_y
    area = jnp.where(live, 0.5 * (first_dx * second_dy - second_dx * first_dy), 1.0)
    half_press = jnp.where(live, 0.2 * ext_l / area, 0.0)
    fa_x, fa_y = -half_press * second_dy, half_press * second_dx
    fb_x, fb_y = half_press * first_dy, -half_press * first_dx

    def gather_force(on_a, on_b):
        total = on_a + rolled(on_b - rolled(on_a, 1, 1), 1, 0) - rolled(on_b, 1, 1)
        return total[:rows, :cols]

    force_x, force_y = gather_force(fa_x, fb_x), gather_force(fa_y, fb_y)
    ratio = jnp.where(
        live[:rows, :cols], jnp.sqrt(area[:rows, :cols]) / jnp.sqrt(0.56 * energy[...]), 1e30
    )
    smallest = jnp.min(jnp.min(ratio, axis=0, keepdims=True), axis=1, keepdims=True)
    early_lane = lax.broadcasted_iota(jnp.int32, (n, 128), 1)
    early[...] = jnp.where(early_lane < 2 * share, early[...], smallest)

    for d in range(1, n_gy):
        pltpu.make_async_remote_copy(
            src_ref=line_slots.at[my], dst_ref=line_slots.at[lax.rem(my + n_gy - d, n_gy)],
            send_sem=line_send_sem.at[d], recv_sem=line_recv_sem.at[d],
            device_id=(mx, lax.rem(my + d, n_gy)), device_id_type=MESH).wait_recv()

    def exchange(sent, landed, send_sem, recv_sem):
        def copy(d, slot):
            target = lax.rem(me + d, n)
            return pltpu.make_async_remote_copy(
                src_ref=sent.at[pl.ds(target, 1)], dst_ref=landed.at[pl.ds(slot, 1)],
                send_sem=send_sem.at[d], recv_sem=recv_sem.at[d],
                device_id=(target // n_gy, lax.rem(target, n_gy)), device_id_type=MESH)

        def start():
            landed[pl.ds(me, 1), :] = sent[pl.ds(me, 1), :]

            def body(d, carry):
                copy(d, me).start()
                return carry
            lax.fori_loop(1, n, body, 0)

        def arrive():
            def body(d, carry):
                copy(d, lax.rem(me + n - d, n)).wait_recv()
                return carry
            lax.fori_loop(1, n, body, 0)

        def drain():
            def body(d, carry):
                copy(d, me).wait_send()
                return carry
            lax.fori_loop(1, n, body, 0)
        return start, arrive, drain

    early_start, early_arrive, early_drain = exchange(early, early_in, early_send_sem, early_recv_sem)
    react_start, react_arrive, react_drain = exchange(react, react_in, react_send_sem, react_recv_sem)
    early_start()

    coords = line_slots[lax.rem(owner, n_gy)].astype(F32)
    shifted = rolled(coords, -1, 1)
    for q, (source, comp) in enumerate([(coords, 0), (coords, 1), (shifted, 0), (shifted, 1)]):
        for h in range(groups):
            table[q * groups + h:q * groups + h + 1, :] = source[comp:comp + 1, h * 128:(h + 1) * 128]
    looked = jnp.dot(table[...].astype(BF16), oh_lo[...], preferred_element_type=F32)
    group_mask = lax.broadcasted_iota(jnp.int32, (groups, pairs), 0) == seg_id // 128
    start_x, start_y, end_x, end_y = [
        jnp.sum(jnp.where(group_mask, looked[q * groups:(q + 1) * groups], 0.0), axis=0, keepdims=True)
        for q in range(4)
    ]
    live_mask = lax.broadcasted_iota(jnp.int32, (1, pairs), 1) < count_ref[0]
    rel_x, rel_y = slave_x - start_x + 0.5, slave_y - start_y
    along_x, along_y = 1.0 + end_x - start_x, end_y - start_y
    along_sq = along_x * along_x + along_y * along_y
    length = jnp.sqrt(along_sq)
    fraction = (rel_x * along_x + rel_y * along_y) / along_sq
    normal_x, normal_y = -along_y / length, along_x / length
    gap_size = normal_x * rel_x + normal_y * rel_y
    side_sign = 1.0 - 2.0 * side[...].astype(F32)
    pressed = -side_sign * gap_size / GAP_SCALE
    soft = jnp.maximum(pressed, 0.0) + jnp.log1p(jnp.exp(-jnp.abs(pressed)))
    magnitude = jnp.where(live_mask, STIFFNESS * GAP_SCALE * soft, 0.0)
    push_x, push_y = magnitude * side_sign * normal_x, magnitude * side_sign * normal_y
    terms = (-push_x, -push_y, magnitude)
    firsts = [two_parts((1.0 - fraction) * t) for t in terms]
    seconds = [two_parts(fraction * t) for t in terms]
    lane_iota = lax.broadcasted_iota(jnp.int32, (share, pairs), 0)
    total = None
    for values, ids, half in ((firsts, seg_id, 0), (seconds, seg_next, 1)):
        lane_mask = lane_iota == ids % share
        for part in range(2):
            spread = jnp.concatenate(
                [jnp.where(lane_mask, values[c][part], 0.0) for c in range(3)]
                + [jnp.zeros((128 - 3 * share, pairs), F32)], axis=0
            ).astype(BF16)
            piece = dot_nt(oh_share[:, half * pairs:(half + 1) * pairs], spread)
            total = piece if total is None else total + piece
    react[...] = total
    react_start()

    (px_top, px_low), (py_top, py_low) = two_parts(push_x), two_parts(push_y)
    placed = jnp.concatenate(
        [jnp.where(row_mask, v, 0.0).astype(BF16) for v in (px_top, py_top, px_low, py_low)], axis=0
    )
    pushed = dot_nt(placed, oh_col[...])
    pushed = pushed[: 2 * rows] + pushed[2 * rows:]
    loads[7].wait()
    loads[8].wait()
    inv_mass = 1.0 / mass[...]
    accel_x = (force_x + pushed[:rows]) * inv_mass
    accel_y = (force_y + pushed[rows:]) * inv_mass

    early_arrive()
    landed = early_in[...]
    prior_sum = jnp.sum(landed, axis=0, keepdims=True)
    lowest = jnp.where(early_lane < 2 * share, 1e30, landed)
    step = 0.3 * jnp.min(jnp.min(lowest, axis=0, keepdims=True), axis=1, keepdims=True)
    for c, accel in enumerate((accel_x, accel_y)):
        speed = vel[c] + step * accel
        new_vel[c] = speed
        new_disp[c] = disp[c] + step * speed
    outs = [pltpu.make_async_copy(new_vel, vel_out, out_sem.at[0]),
            pltpu.make_async_copy(new_disp, disp_out, out_sem.at[1])]
    for out in outs:
        out.start()

    react_arrive()
    react_sum = step * jnp.sum(react_in[...], axis=0, keepdims=True)
    for c in range(3):
        piece = react_sum[:, c * share:(c + 1) * share]
        if c < 2:
            piece = piece + prior_sum[:, c * share:(c + 1) * share]
        new_imp[c:c + 1, :] = piece
    last_out = pltpu.make_async_copy(new_imp, imp_out, out_sem.at[2])
    last_out.start()

    for copy in plane_copies + line_copies:
        copy.wait_send()

    @pl.when(has_up)
    def _():
        to_up.wait_send()

    @pl.when(has_down)
    def _():
        to_down.wait_send()

    @pl.when(has_left)
    def _():
        to_left.wait_send()

    @pl.when(has_right)
    def _():
        to_right.wait_send()

    early_drain()
    react_drain()
    for out in outs + [last_out]:
        out.wait()


def shards(n_gx, n_gy, node_disp, node_vel, node_mass, zone_mass, zone_energy, master_block, owner,
           pair_node, pair_segment, pair_side, pair_count):
    n = n_gx * n_gy
    rows, cols = node_mass.shape
    pairs = pair_node.shape[1]
    mnodes = master_block.shape[2]
    share = mnodes // n
    any_spec = pl.BlockSpec(memory_space=pl.ANY)
    smem = pl.BlockSpec(memory_space=pltpu.SMEM)
    vm = pltpu.VMEM
    dma = pltpu.SemaphoreType.DMA
    i32 = jnp.int32
    return pl.pallas_call(
        functools.partial(step_kernel, n_gx, n_gy),
        out_shape=(
            jax.ShapeDtypeStruct((2, rows, cols), F32),
            jax.ShapeDtypeStruct((2, rows, cols), F32),
            jax.ShapeDtypeStruct((3, share), F32),
        ),
        in_specs=[smem, smem] + [any_spec] * 9,
        out_specs=(any_spec,) * 3,
        scratch_shapes=[
            vm((2, rows, cols), F32), vm((2, rows, cols), F32), vm((rows, cols), F32), vm((rows, cols), F32),
            vm((rows, cols), F32), vm((1, 4, mnodes), BF16), vm((1, pairs), i32), vm((1, pairs), i32),
            vm((1, pairs), i32),
            vm((2, rows, cols), F32), vm((2, rows, cols), F32), vm((3, share), F32),
            vm((8, cols), F32), vm((8, cols), F32), vm((rows + 8, 128), F32), vm((rows + 8, 128), F32),
            vm((8, cols), F32), vm((8, cols), F32), vm((rows + 8, 128), F32), vm((rows + 8, 128), F32),
            vm((n_gx, 2, mnodes), BF16), vm((2, mnodes), BF16), vm((n_gy, 2, mnodes), BF16),
            vm((4 * (mnodes // 128), 128), F32),
            vm((cols, pairs), BF16), vm((128, pairs), BF16), vm((n, 2 * pairs), BF16),
            vm((n, 128), F32), vm((n, 128), F32), vm((n, 128), F32), vm((n, 128), F32),
            dma((9,)), dma((3,)), dma((4,)), dma((4,)),
            dma((n_gx,)), dma((n_gx,)), dma((n_gy,)), dma((n_gy,)),
            dma((n,)), dma((n,)), dma((n,)), dma((n,)),
        ],
        compiler_params=pltpu.CompilerParams(collective_id=0, has_side_effects=True),
    )(owner, pair_count, node_disp, node_vel, node_mass, zone_mass, zone_energy, master_block,
      pair_node, pair_segment, pair_side)


def solution(mesh):
    in_specs = (
        P(None, "gx", "gy"), P(None, "gx", "gy"), P("gx", "gy"), P("gx", "gy"), P("gx", "gy"),
        P(("gx", "gy"), None, None), P(), P(("gx", "gy"), None), P(("gx", "gy"), None),
        P(("gx", "gy"), None), P(("gx", "gy")),
    )
    out_specs = (P(None, "gx", "gy"), P(None, "gx", "gy"), P(None, ("gx", "gy")))
    body = functools.partial(shards, mesh.shape["gx"], mesh.shape["gy"])
    return jax.shard_map(body, mesh=mesh, in_specs=in_specs, out_specs=out_specs, check_vma=False)
```

time: 288 us -> 25.1 us (0.09)
  blocking collectives: 222 us -> 0 us
  other arithmetic: 29 us -> 0 us
  Pallas kernels: 0 us -> 20.2 us
  local copies, waits for them, and re-layouts: 18.4 us -> 2.75 us
  starting transfers between devices: 7.77 us -> 0 us
  waiting for transfers between devices: 4.41 us -> 0 us
    psum x2 -> x0, blocking collectives: 182 us -> none  [the longest x1 138 us: shards(): summed = lax.psum(reaction, ('gx', 'gy'))]
    pmin x1 -> x0, blocking collectives: 40.6 us -> none  [shards(): step_size = 0.3 * lax.pmin(jnp.min(zone_ratio), ('gx', 'gy'))]
    pallas_call x0 -> x1, Pallas kernels: none -> 20.2 us  [shards(): pl.pallas_call(functools.partial(step_kernel, n_gx, n_gy), out_shape=(jax...]
    scatter-add x6 -> x0, other arithmetic: 16.4 us -> none  [the longest x2 10.6 us: contact_block(): pushed = pushed.at[:, slave_nodes].add(slave_push)]
    gather x12 -> x0, local copies, waits for them, and re-layouts: 8.6 us -> none  [the longest x4 5.79 us: contact_block(): slave_disp = jnp.take(flat_disp, slave_nodes, axis=1)]
    ppermute x4 -> x0, starting transfers between devices: 7.77 us -> none  [the longest x2 5.19 us: with_halo(): lax.ppermute(tail, axis, [(i, (i + 1) % count) for i in range(ends)])]
    ppermute x4 -> x0, waiting for transfers between devices: 4.41 us -> none  [the longest x2 4.23 us: with_halo(): lax.ppermute(head, axis, [((i + 1) % count, i) for i in range(ends)])]
    mul x9 -> x0, other arithmetic: 4.34 us -> none  [the longest x2 2.71 us: contact_terms(): -fraction * slave_push[0]]
  transfers between devices with their start and end apart: 4 -> 0, of which waited for: 2 -> 0; matrix products, arithmetic and copies ran while one was open for 14% -> 0% of each run, Pallas kernels for 0% -> 0%
where the time goes in v1:
time: 25.1 us; the launch traced here: 24.9 us
  Pallas kernels  20.2 us (80%)
  local copies, waits for them, and re-layouts  2.75 us (11%)
  between operations  1.94 us (8%)
    pallas_call x1, Pallas kernels, shards(): pl.pallas_call(functools.partial(step_kernel, n_gx, n_gy), out_shape=(jax...  20.2 us
    unnamed x7, local copies, waits for them, and re-layouts  2.75 us

profile of v1, /device:TPU:0, one launch (start us, length us, event | category | flops | bytes accessed | tf_op | source)
XLA Modules:
  0.0 24.9 jit_solution(16707216805612294327)
XLA Ops:
  1.9 20.2 %shard_map.130 = (f32[2,32,256]{2,1,0:T(8,128)}, f32[2,32,256]{2,1,0:T(8,128)}, f32[3,32]{1,0:T(4,128)}) custom-call(s32[1]{0:T(128)S(6)} %copy.17.owner_ref, s32[1]{0:T(128)S(6)} %copy.18.count_ref, f32[2,32,256]{2,1,0:T(8,128)} %disp_in.1, f32[2,32,256]{2,1,0:T(8,128)} %vel_in.1, f32[32,256]{1,0:T(8,128)} %mass_in.1, f32[32,256]{1,0:T(8,128)} %zmass_in.1, ...), custom_call_target="tpu_custom_call" | custom-call | tf_op jit(solution)/shard_map/pallas_call | solution.py:383
  22.1 0.0 copy-start
  22.1 1.5 %copy.19 = f32[2,32,256]{2,1,0:T(8,128)} copy(f32[2,32,256]{2,1,0:T(8,128)} %get-tuple-element.6) | data formatting | bytes 131072
  23.6 0.0 copy-done
  23.6 0.0 copy-start.1
  23.6 0.6 %copy.20 = f32[2,32,256]{2,1,0:T(8,128)} copy(f32[2,32,256]{2,1,0:T(8,128)S(1)} %copy-done) | data formatting | bytes 131072
  24.3 0.0 copy-done.1
  24.3 0.6 %copy.21 = f32[3,32]{1,0:T(4,128)} copy(f32[3,32]{1,0:T(4,128)S(1)} %copy-done.1) | data formatting | bytes 768
Async XLA Ops:
  22.1 1.5 %copy-start = (f32[2,32,256]{2,1,0:T(8,128)S(1)}, f32[2,32,256]{2,1,0:T(8,128)}, u32[]{:S(2)}) copy-start(f32[2,32,256]{2,1,0:T(8,128)} %get-tuple-element.7) | copy-start | bytes 196612
  23.6 0.7 %copy-start.1 = (f32[3,32]{1,0:T(4,128)S(1)}, f32[3,32]{1,0:T(4,128)}, u32[]{:S(2)}) copy-start(f32[3,32]{1,0:T(4,128)} %get-tuple-element.8) | copy-start | bytes 1156

commit v2 on v1

--- a/solution.py
+++ b/solution.py
@@ -29,15 +29,14 @@
 
 def step_kernel(
     n_gx, n_gy,
-    owner_ref, count_ref, disp_in, vel_in, mass_in, zmass_in, energy_in, block_in, node_in, seg_in, side_in,
-    vel_out, disp_out, imp_out,
-    disp, vel, mass, zmass, energy, block, node, seg, side,
+    owner_in, count_in, disp_in, vel_in, mass_in, zmass_in, energy_in, block_in, node_in, seg_in, side_in,
     new_vel, new_disp, new_imp,
+    owner_ref, count_ref, disp, vel, mass, zmass, energy, block, node, seg, side,
     up_pack, down_pack, left_pack, right_pack,
     from_down, from_up, from_right, from_left,
-    plane_slots, line_send, line_slots, table,
+    plane_slots, line_slots, table,
     oh_col, oh_lo, oh_share, early, early_in, react, react_in,
-    in_sem, out_sem, halo_send, halo_recv,
+    in_sem, halo_send, halo_recv,
     plane_send_sem, plane_recv_sem, line_send_sem, line_recv_sem,
     early_send_sem, early_recv_sem, react_send_sem, react_recv_sem,
 ):
@@ -54,7 +53,7 @@
         pltpu.make_async_copy(src, dst, in_sem.at[i])
         for i, (src, dst) in enumerate(
             [(block_in, block), (node_in, node), (disp_in, disp), (seg_in, seg), (energy_in, energy),
-             (zmass_in, zmass), (side_in, side), (mass_in, mass), (vel_in, vel)]
+             (zmass_in, zmass), (side_in, side), (owner_in, owner_ref), (count_in, count_ref), (mass_in, mass), (vel_in, vel)]
         )
     ]
     for load in loads:
@@ -68,7 +67,7 @@
     for d in range(1, n_gy):
         pl.semaphore_signal(barrier, inc=1, device_id=(mx, lax.rem(my + d, n_gy)), device_id_type=MESH)
 
-    for load in loads[:7]:
+    for load in loads[:9]:
         load.wait()
 
     dx, dy = disp[0], disp[1]
@@ -80,7 +79,11 @@
         sub == 7, dx[tail],
         jnp.where(sub == 6, rolled(dy[tail], -1, 0), jnp.where(sub == 5, rolled(zload[tail], -2, 0), 0.0)),
     )
-    plane_slots[mx] = block[0, 0:2]
+    own = block[0, 0:2].astype(F32)
+    for c in range(2):
+        for h in range(groups):
+            table[c * groups + h:c * groups + h + 1, :] = own[c:c + 1, h * 128:(h + 1) * 128]
+    plane_slots[mx] = table[...].astype(BF16)
 
     node_id = node[...]
     seg_id = seg[...]
@@ -142,6 +145,21 @@
     @pl.when(has_down)
     def _():
         to_down.start()
+
+    for d in range(1, n_gx):
+        pltpu.make_async_remote_copy(
+            src_ref=plane_slots.at[mx], dst_ref=plane_slots.at[lax.rem(mx + n_gx - d, n_gx)],
+            send_sem=plane_send_sem.at[d], recv_sem=plane_recv_sem.at[d],
+            device_id=(lax.rem(mx + d, n_gx), my), device_id_type=MESH).wait_recv()
+
+    line_slots[my] = plane_slots[owner // n_gy]
+    line_copies = []
+    for d in range(1, n_gy):
+        line_copies.append(pltpu.make_async_remote_copy(
+            src_ref=line_slots.at[my], dst_ref=line_slots.at[my],
+            send_sem=line_send_sem.at[d], recv_sem=line_recv_sem.at[d],
+            device_id=(mx, lax.rem(my + d, n_gy)), device_id_type=MESH))
+        line_copies[-1].start()
 
     @pl.when(has_down)
     def _():
@@ -171,21 +189,6 @@
     @pl.when(has_right)
     def _():
         to_right.start()
-
-    for d in range(1, n_gx):
-        pltpu.make_async_remote_copy(
-            src_ref=plane_slots.at[mx], dst_ref=plane_slots.at[lax.rem(mx + n_gx - d, n_gx)],
-            send_sem=plane_send_sem.at[d], recv_sem=plane_recv_sem.at[d],
-            device_id=(lax.rem(mx + d, n_gx), my), device_id_type=MESH).wait_recv()
-
-    line_slots[my] = plane_slots[owner // n_gy]
-    line_copies = []
-    for d in range(1, n_gy):
-        line_copies.append(pltpu.make_async_remote_copy(
-            src_ref=line_slots.at[my], dst_ref=line_slots.at[my],
-            send_sem=line_send_sem.at[d], recv_sem=line_recv_sem.at[d],
-            device_id=(mx, lax.rem(my + d, n_gy)), device_id_type=MESH))
-        line_copies[-1].start()
 
     @pl.when(has_right)
     def _():
@@ -268,10 +271,11 @@
 
     coords = line_slots[lax.rem(owner, n_gy)].astype(F32)
     shifted = rolled(coords, -1, 1)
-    for q, (source, comp) in enumerate([(coords, 0), (coords, 1), (shifted, 0), (shifted, 1)]):
-        for h in range(groups):
-            table[q * groups + h:q * groups + h + 1, :] = source[comp:comp + 1, h * 128:(h + 1) * 128]
-    looked = jnp.dot(table[...].astype(BF16), oh_lo[...], preferred_element_type=F32)
+    last_lane = lax.broadcasted_iota(jnp.int32, coords.shape, 1) == 127
+    shifted = jnp.where(last_lane, rolled(shifted, -1, 0), shifted)
+    looked = jnp.dot(
+        jnp.concatenate([coords, shifted], axis=0).astype(BF16), oh_lo[...], preferred_element_type=F32
+    )
     group_mask = lax.broadcasted_iota(jnp.int32, (groups, pairs), 0) == seg_id // 128
     start_x, start_y, end_x, end_y = [
         jnp.sum(jnp.where(group_mask, looked[q * groups:(q + 1) * groups], 0.0), axis=0, keepdims=True)
@@ -313,8 +317,8 @@
     )
     pushed = dot_nt(placed, oh_col[...])
     pushed = pushed[: 2 * rows] + pushed[2 * rows:]
-    loads[7].wait()
-    loads[8].wait()
+    loads[9].wait()
+    loads[10].wait()
     inv_mass = 1.0 / mass[...]
     accel_x = (force_x + pushed[:rows]) * inv_mass
     accel_y = (force_y + pushed[rows:]) * inv_mass
@@ -328,10 +332,6 @@
         speed = vel[c] + step * accel
         new_vel[c] = speed
         new_disp[c] = disp[c] + step * speed
-    outs = [pltpu.make_async_copy(new_vel, vel_out, out_sem.at[0]),
-            pltpu.make_async_copy(new_disp, disp_out, out_sem.at[1])]
-    for out in outs:
-        out.start()
 
     react_arrive()
     react_sum = step * jnp.sum(react_in[...], axis=0, keepdims=True)
@@ -340,8 +340,6 @@
         if c < 2:
             piece = piece + prior_sum[:, c * share:(c + 1) * share]
         new_imp[c:c + 1, :] = piece
-    last_out = pltpu.make_async_copy(new_imp, imp_out, out_sem.at[2])
-    last_out.start()
 
     for copy in plane_copies + line_copies:
         copy.wait_send()
@@ -364,8 +362,17 @@
 
     early_drain()
     react_drain()
-    for out in outs + [last_out]:
-        out.wait()
+
+
+def write_kernel(vel, disp, imp, vel_out, disp_out, imp_out, sem):
+    copies = [
+        pltpu.make_async_copy(src, dst, sem.at[i])
+        for i, (src, dst) in enumerate([(vel, vel_out), (disp, disp_out), (imp, imp_out)])
+    ]
+    for copy in copies:
+        copy.start()
+    for copy in copies:
+        copy.wait()
 
 
 def shards(n_gx, n_gy, node_disp, node_vel, node_mass, zone_mass, zone_energy, master_block, owner,
@@ -375,38 +382,45 @@
     pairs = pair_node.shape[1]
     mnodes = master_block.shape[2]
     share = mnodes // n
-    any_spec = pl.BlockSpec(memory_space=pl.ANY)
-    smem = pl.BlockSpec(memory_space=pltpu.SMEM)
+    groups = mnodes // 128
+    any_spec = pl.BlockSpec(memory_space=pltpu.HBM)
+    vmem_spec = pl.BlockSpec(memory_space=pltpu.VMEM)
+    smem = pltpu.SMEM
     vm = pltpu.VMEM
     dma = pltpu.SemaphoreType.DMA
     i32 = jnp.int32
-    return pl.pallas_call(
+    kept = pl.pallas_call(
         functools.partial(step_kernel, n_gx, n_gy),
         out_shape=(
-            jax.ShapeDtypeStruct((2, rows, cols), F32),
-            jax.ShapeDtypeStruct((2, rows, cols), F32),
-            jax.ShapeDtypeStruct((3, share), F32),
+            vm((2, rows, cols), F32), vm((2, rows, cols), F32), vm((3, share), F32),
         ),
-        in_specs=[smem, smem] + [any_spec] * 9,
-        out_specs=(any_spec,) * 3,
+        in_specs=[any_spec] * 11,
+        out_specs=(vmem_spec,) * 3,
         scratch_shapes=[
+            smem((1,), i32), smem((1,), i32),
             vm((2, rows, cols), F32), vm((2, rows, cols), F32), vm((rows, cols), F32), vm((rows, cols), F32),
             vm((rows, cols), F32), vm((1, 4, mnodes), BF16), vm((1, pairs), i32), vm((1, pairs), i32),
             vm((1, pairs), i32),
-            vm((2, rows, cols), F32), vm((2, rows, cols), F32), vm((3, share), F32),
             vm((8, cols), F32), vm((8, cols), F32), vm((rows + 8, 128), F32), vm((rows + 8, 128), F32),
             vm((8, cols), F32), vm((8, cols), F32), vm((rows + 8, 128), F32), vm((rows + 8, 128), F32),
-            vm((n_gx, 2, mnodes), BF16), vm((2, mnodes), BF16), vm((n_gy, 2, mnodes), BF16),
-            vm((4 * (mnodes // 128), 128), F32),
+            vm((n_gx, 2 * groups, 128), BF16), vm((n_gy, 2 * groups, 128), BF16),
+            vm((2 * groups, 128), F32),
             vm((cols, pairs), BF16), vm((128, pairs), BF16), vm((n, 2 * pairs), BF16),
             vm((n, 128), F32), vm((n, 128), F32), vm((n, 128), F32), vm((n, 128), F32),
-            dma((9,)), dma((3,)), dma((4,)), dma((4,)),
+            dma((11,)), dma((4,)), dma((4,)),
             dma((n_gx,)), dma((n_gx,)), dma((n_gy,)), dma((n_gy,)),
             dma((n,)), dma((n,)), dma((n,)), dma((n,)),
         ],
         compiler_params=pltpu.CompilerParams(collective_id=0, has_side_effects=True),
     )(owner, pair_count, node_disp, node_vel, node_mass, zone_mass, zone_energy, master_block,
       pair_node, pair_segment, pair_side)
+    return pl.pallas_call(
+        write_kernel,
+        out_shape=tuple(jax.ShapeDtypeStruct(k.shape, k.dtype) for k in kept),
+        in_specs=[vmem_spec] * 3,
+        out_specs=(any_spec,) * 3,
+        scratch_shapes=[dma((3,))],
+    )(*[pltpu.with_memory_space_constraint(k, pltpu.VMEM) for k in kept])
 
 
 def solution(mesh):

time: 25.1 us -> 22.8 us (0.908)
  local copies, waits for them, and re-layouts: 2.75 us -> 0 us
  Pallas kernels: 20.2 us -> 20.7 us
    unnamed x7 -> x0, local copies, waits for them, and re-layouts: 2.75 us -> none
    pallas_call x1 -> x2, Pallas kernels: 20.2 us -> 20.7 us  [the longest x1 20 us: shards(): pl.pallas_call(functools.partial(step_kernel, n_gx, n_gy), out_shape=(vm(...]
where the time goes in v2:
time: 22.8 us; the launch traced here: 22.6 us
  Pallas kernels  20.7 us (91%)
  between operations  1.93 us (8%)
    pallas_call x1, Pallas kernels, shards(): pl.pallas_call(functools.partial(step_kernel, n_gx, n_gy), out_shape=(vm(...  20 us
    pallas_call x1, Pallas kernels, shards(): pl.pallas_call(write_kernel, out_shape=tuple((jax.ShapeDtypeStruct(k.shap...  0.68 us

profile of v2, /device:TPU:0, one launch (start us, length us, event | category | flops | bytes accessed | tf_op | source)
XLA Modules:
  0.0 22.6 jit_solution(14169637587004805692)
XLA Ops:
  1.9 20.0 %shard_map.130 = (f32[2,32,256]{2,1,0:T(8,128)S(1)}, f32[2,32,256]{2,1,0:T(8,128)S(1)}, f32[3,32]{1,0:T(4,128)S(1)}) custom-call(s32[1]{0:T(128)S(6)} %copy.14.owner_in, s32[1]{0:T(128)S(6)} %copy.15.count_in, f32[2,32,256]{2,1,0:T(8,128)} %disp_in.1, f32[2,32,256]{2,1,0:T(8,128)} %vel_in.1, f32[32,256]{1,0:T(8,128)} %mass_in.1, f32[32,256]{1,0:T(8,128)} %zmass_in.1, ...), custom_call_target="tpu_custom_call" | custom-call | tf_op jit(solution)/shard_map/pallas_call | solution.py:392
  21.9 0.7 %shard_map.131 = (f32[2,32,256]{2,1,0:T(8,128)}, f32[2,32,256]{2,1,0:T(8,128)}, f32[3,32]{1,0:T(4,128)}) custom-call(f32[2,32,256]{2,1,0:T(8,128)S(1)} %get-tuple-element.6.vel, f32[2,32,256]{2,1,0:T(8,128)S(1)} %get-tuple-element.7.disp, f32[3,32]{1,0:T(4,128)S(1)} %get-tuple-element.8.imp), custom_call_target="tpu_custom_call" | custom-call | tf_op jit(solution)/shard_map/pallas_call | solution.py:417

commit v3 on v2

--- a/solution.py
+++ b/solution.py
@@ -250,19 +250,19 @@
             def body(d, carry):
                 copy(d, me).start()
                 return carry
-            lax.fori_loop(1, n, body, 0)
+            lax.fori_loop(1, n, body, 0, unroll=n <= 64)
 
         def arrive():
             def body(d, carry):
                 copy(d, lax.rem(me + n - d, n)).wait_recv()
                 return carry
-            lax.fori_loop(1, n, body, 0)
+            lax.fori_loop(1, n, body, 0, unroll=n <= 64)
 
         def drain():
             def body(d, carry):
                 copy(d, me).wait_send()
                 return carry
-            lax.fori_loop(1, n, body, 0)
+            lax.fori_loop(1, n, body, 0, unroll=n <= 64)
         return start, arrive, drain
 
     early_start, early_arrive, early_drain = exchange(early, early_in, early_send_sem, early_recv_sem)

time: 22.8 us -> 22 us (0.965)
  Pallas kernels: 20.7 us -> 19.9 us
    pallas_call x1, Pallas kernels: 20 us -> 19.2 us  [shards(): pl.pallas_call(functools.partial(step_kernel, n_gx, n_gy), out_shape=(vm(...]
where the time goes in v3:
time: 22 us; the launch traced here: 21.8 us
  Pallas kernels  19.9 us (90%)
  between operations  1.93 us (9%)
    pallas_call x1, Pallas kernels, shards(): pl.pallas_call(functools.partial(step_kernel, n_gx, n_gy), out_shape=(vm(...  19.2 us
    pallas_call x1, Pallas kernels, shards(): pl.pallas_call(write_kernel, out_shape=tuple((jax.ShapeDtypeStruct(k.shap...  0.68 us

profile of v3, /device:TPU:0, one launch (start us, length us, event | category | flops | bytes accessed | tf_op | source)
XLA Modules:
  0.0 21.8 jit_solution(14417772849047224160)
XLA Ops:
  1.9 19.2 %shard_map.130 = (f32[2,32,256]{2,1,0:T(8,128)S(1)}, f32[2,32,256]{2,1,0:T(8,128)S(1)}, f32[3,32]{1,0:T(4,128)S(1)}) custom-call(s32[1]{0:T(128)S(6)} %copy.14.owner_in, s32[1]{0:T(128)S(6)} %copy.15.count_in, f32[2,32,256]{2,1,0:T(8,128)} %disp_in.1, f32[2,32,256]{2,1,0:T(8,128)} %vel_in.1, f32[32,256]{1,0:T(8,128)} %mass_in.1, f32[32,256]{1,0:T(8,128)} %zmass_in.1, ...), custom_call_target="tpu_custom_call" | custom-call | tf_op jit(solution)/shard_map/pallas_call | solution.py:392
  21.1 0.7 %shard_map.131 = (f32[2,32,256]{2,1,0:T(8,128)}, f32[2,32,256]{2,1,0:T(8,128)}, f32[3,32]{1,0:T(4,128)}) custom-call(f32[2,32,256]{2,1,0:T(8,128)S(1)} %get-tuple-element.6.vel, f32[2,32,256]{2,1,0:T(8,128)S(1)} %get-tuple-element.7.disp, f32[3,32]{1,0:T(4,128)S(1)} %get-tuple-element.8.imp), custom_call_target="tpu_custom_call" | custom-call | tf_op jit(solution)/shard_map/pallas_call | solution.py:417
